TPU v7x, 32 devices: a whole 2x2x4 slice. The times are simulated.
32 devices in a mesh: groups: 2 (over x), expert: 16 (over z, y, core).
Axes of the slice: x: 2, y: 2, z: 4, core: 2. Of those that a mesh axis runs over, the one named last changes fastest.
Arguments:
- queries: bfloat16 [256, 4096], P(('groups', 'expert')), parts along dimension 0, may hold values from -150 to 150
- key_cache: bfloat16 [256, 64, 512], P(('groups', 'expert')), parts along dimension 0, may hold values from -7 to 7
- value_cache: bfloat16 [256, 64, 512], P(('groups', 'expert')), parts along dimension 0, may hold values from -6 to 6
- new_key: bfloat16 [256, 512], P(('groups', 'expert')), parts along dimension 0, may hold values from -6 to 6
- new_value: bfloat16 [256, 512], P(('groups', 'expert')), parts along dimension 0, may hold values from -6 to 6
- cache_lengths: int32 [256], P(('groups', 'expert')), parts along dimension 0, may hold values from 2 to 64, as said below
- hidden_in: bfloat16 [2048, 2048], P(('groups', 'expert')), parts along dimension 0, may hold values from -6 to 6
- norm_gain: bfloat16 [2048], replicated, may hold values from 0.5 to 1.5
- router_weight: bfloat16 [2048, 16], replicated, may hold values from -0.125 to 0.125
- expert_ids: int32 [2048, 8], P(('groups', 'expert')), parts along dimension 0, may hold values from 0 to 15, all different within a row; in each aligned block of 64 rows (0 to 63, 64 to 127, ...) at most 64 rows name the same one
- gate_train: bfloat16 [16, 2048, 768], P(None, 'expert'), may hold values from -0.125 to 0.125
- up_train: bfloat16 [16, 2048, 768], P(None, 'expert'), may hold values from -0.125 to 0.125
- down_train: bfloat16 [16, 768, 2048], P(None, 'expert'), may hold values from -0.21875 to 0.21875
Outputs:
- attended: bfloat16 [256, 4096], P(('groups', 'expert')), parts along dimension 0
- expert_mix: bfloat16 [2048, 2048], P(('groups', 'expert')), parts along dimension 0
There are 2 independent parts, one for each index of `groups`. A program takes and returns all parts, laid end to end along the dimension named above; an argument that names none is the same for every part. Nothing has to cross between parts.
Inputs may be any that keep to these rules, and one draw needn't show every extreme that they name: `expert_ids`: each row names 8 different experts; within the rows of one device no expert is named more than 64 times. `cache_lengths`: the first sequence of each device's 8 has all 64 positions filled.
All inputs are finite; a program needn't handle non-finite values.
Results may differ from a plain program's by a relative error of at most 0.0074.
Values may be sent and summed in bfloat16 or wider, within the bound.
A program may use at most 128 MiB of HBM per device.

v0:
```python
import functools
import math

import jax
import jax.numpy as jnp
from jax import lax
from jax.experimental import pallas as pl
from jax.experimental.pallas import tpu as pltpu
from jax.sharding import PartitionSpec as P

HEADS = 32
KV_HEADS = 4
HEAD_DIM = 128
CTX = 64


EPSILON = 1e-06


def rms_normed(hidden_in, norm_gain):
    values = hidden_in.astype(jnp.float32)
    mean_square = jnp.mean(values * values, axis=-1, keepdims=True)
    return (values * lax.rsqrt(mean_square + EPSILON) * norm_gain.astype(jnp.float32)).astype(
        jnp.bfloat16
    )


def attend(queries, key_cache, value_cache, new_key, new_value, cache_lengths):
    seq_count = queries.shape[0]
    group_size = HEADS // KV_HEADS
    query_blocks = queries.reshape(seq_count, KV_HEADS, group_size, HEAD_DIM)
    cached_keys = key_cache.reshape(seq_count, CTX, KV_HEADS, HEAD_DIM)
    cached_values = value_cache.reshape(seq_count, CTX, KV_HEADS, HEAD_DIM)
    fresh_keys = new_key.reshape(seq_count, KV_HEADS, HEAD_DIM)
    fresh_values = new_value.astype(jnp.float32).reshape(seq_count, KV_HEADS, HEAD_DIM)
    score_scale = 1.0 / math.sqrt(HEAD_DIM)
    scores = (
        jnp.einsum("sgrd,scgd->sgrc", query_blocks, cached_keys, preferred_element_type=jnp.float32)
        * score_scale
    )
    own_score = (
        jnp.einsum("sgrd,sgd->sgr", query_blocks, fresh_keys, preferred_element_type=jnp.float32)
        * score_scale
    )
    positions = jnp.arange(CTX, dtype=jnp.int32)
    visible = positions[None, :] < cache_lengths[:, None]
    scores = jnp.where(visible[:, None, None, :], scores, -1e30)
    largest = jnp.maximum(jnp.max(scores, axis=-1), own_score)
    cached_exp = jnp.exp(scores - largest[..., None])
    own_exp = jnp.exp(own_score - largest)
    prob_total = jnp.sum(cached_exp, axis=-1) + own_exp
    cached_prob = (cached_exp / prob_total[..., None]).astype(jnp.bfloat16)
    own_prob = (own_exp / prob_total).astype(jnp.bfloat16).astype(jnp.float32)
    context = jnp.einsum(
        "sgrc,scgd->sgrd", cached_prob, cached_values, preferred_element_type=jnp.float32
    )
    context = context + own_prob[..., None] * fresh_values[:, :, None, :]
    return context.reshape(seq_count, HEADS * HEAD_DIM).astype(jnp.bfloat16)


def dense_mixing(normed, router_weight, expert_ids):
    logits = jnp.dot(normed, router_weight, preferred_element_type=jnp.float32)
    expert_range = jnp.arange(router_weight.shape[1], dtype=jnp.int32)
    picked = jnp.any(expert_ids[:, :, None] == expert_range[None, None, :], axis=1)
    masked = jnp.where(picked, logits, -jnp.inf)
    raised = jnp.exp(masked - jnp.max(masked, axis=-1, keepdims=True))
    return raised / jnp.sum(raised, axis=-1, keepdims=True)


MESH = pl.DeviceIdType.MESH
AHEAD = 4
NEAR = 4


def greet(targets):
    barrier = pltpu.get_barrier_semaphore()

    expected = 0
    for condition, target in targets:
        signal = functools.partial(
            pl.semaphore_signal, barrier, inc=1, device_id=target, device_id_type=MESH
        )
        if condition is None:
            signal()
            expected = expected + 1
        else:
            pl.when(condition)(signal)
            expected = expected + condition.astype(jnp.int32)
    pl.semaphore_wait(barrier, expected)


def move_kernel(
    groups, count,
    gate_ref, up_ref, down_ref, rows_ref,
    hidden_ref, down_out, gate_out, up_out, rows_out,
    send_w, recv_w, send_x, recv_x, local_sem, send_rows, recv_rows,
):
    me = lax.axis_index("expert")
    group = lax.axis_index("groups")
    parts = max(1, groups // 2)
    part_rows = gate_ref.shape[1] // parts
    part_columns = down_ref.shape[2] // groups
    line = count // 4
    layer = me // 4

    others = [(None, (group, me ^ r)) for r in range(1, count)]
    others += [(None, (lax.rem(group + h, groups), me)) for h in range(1, groups)]
    greet(others)

    def remote(src, dst, send, recv, target):
        return pltpu.make_async_remote_copy(
            src_ref=src, dst_ref=dst, send_sem=send, recv_sem=recv, device_id=target, device_id_type=MESH
        )

    def rows_of(owner):
        return pl.ds(pl.multiple_of((owner // 2) * part_rows, part_rows), part_rows)

    def columns_of(owner):
        return pl.ds(pl.multiple_of(owner * part_columns, part_columns), part_columns)

    def row_copy(kind, block, target, own=False):
        source = rows_ref if own else rows_out.at[block]
        return remote(
            source, rows_out.at[block], send_rows.at[kind, block], recv_rows.at[block], (group, target)
        )

    def row_wait(block):
        row_copy(0, block, me ^ 1).wait_recv()

    own_rows = pltpu.make_async_copy(rows_ref, rows_out.at[me], local_sem.at[3])
    own_rows.start()
    has_up, has_down = me + 4 < count, me >= 4

    @pl.when(has_up)
    def _():
        row_copy(0, me, me + 4, True).start()

    @pl.when(has_down)
    def _():
        row_copy(1, me, me - 4, True).start()

    row_copy(2, me, me ^ 2, True).start()
    row_copy(3, me, me ^ 1, True).start()

    def line_step(step):
        below, above = me - 4 * (step + 1), me + 4 * (step + 1)

        @pl.when(below >= 0)
        def _():
            row_wait(below)

            @pl.when(has_up)
            def _():
                row_copy(0, below, me + 4).start()

            row_copy(2, below, me ^ 2).start()
            row_copy(3, below, me ^ 1).start()

        @pl.when(above < count)
        def _():
            row_wait(above)

            @pl.when(has_down)
            def _():
                row_copy(1, above, me - 4).start()

            row_copy(2, above, me ^ 2).start()
            row_copy(3, above, me ^ 1).start()

    def side_step(index):
        block = lax.rem(me, 4) ^ 2
        block = block + 4 * index
        row_wait(block)
        row_copy(3, block, me ^ 1).start()

    def across(kind, r, refs_in, refs_out, which):
        target = me ^ r
        if r < NEAR:
            a, b = ((gate_ref, gate_out), (down_ref, down_out), (up_ref, up_out))[kind]
            send = send_x.at[0, r, 0] if kind == 2 else send_w.at[kind, r]
            recv = recv_x.at[0, r, 0] if kind == 2 else recv_w.at[kind, r]
            return remote(a.at[target], b.at[me], send, recv, (group, target))
        if kind == 0:
            return remote(
                refs_in[which].at[target, rows_of(group)], refs_out[which].at[me, rows_of(group)],
                send_w.at[0, r], recv_w.at[0, r], (group, target),
            )
        return remote(
            down_ref.at[target, :, columns_of(group)], down_out.at[me, :, columns_of(group)],
            send_w.at[1, r], recv_w.at[1, r], (group, target),
        )

    ins, outs = (gate_ref, up_ref), (gate_out, up_out)

    def by_matrix(act):
        pl.when(lax.rem(group, 2) == 0)(functools.partial(act, 0))
        pl.when(lax.rem(group, 2) == 1)(functools.partial(act, 1))

    def start_weight(kind, r):
        if kind == 0 and r >= NEAR:
            by_matrix(lambda which: across(0, r, ins, outs, which).start())
        else:
            across(kind, r, ins, outs, 0).start()

    def onward(kind, r, h, which):
        held = me ^ r
        place = outs[which].at[held, rows_of(group)] if kind == 0 else down_out.at[held, :, columns_of(group)]
        return remote(
            place, place, send_x.at[kind, r, h - 1], recv_x.at[kind, r, h - 1],
            (lax.rem(group + h, groups), me),
        )

    def pass_on(kind, r):
        across(kind, r, ins, outs, 0).wait_recv()
        for h in range(1, groups if r >= NEAR else 1):
            if kind == 0:
                by_matrix(lambda which: onward(0, r, h, which).start())
            else:
                onward(1, r, h, 0).start()

    own_copies = [
        pltpu.make_async_copy(a.at[me], b.at[me], local_sem.at[i])
        for i, (a, b) in enumerate(((gate_ref, gate_out), (up_ref, up_out), (down_ref, down_out)))
    ]
    width = gate_ref.shape[1] * count

    def ready():
        for index in range(line):
            for y in range(2):
                row_wait(4 * index + 2 * y + (lax.rem(me, 2) ^ 1))
        own_rows.wait()
        for copy in own_copies[:2]:
            copy.wait()
        for r in order:
            for h in range(1, groups if r >= NEAR else 1):
                onward(0, r, h, 0).wait_recv()

    def expert_rows(quarter):
        @pl.loop(0, count // 16)
        def _(step):
            at = quarter * (count // 4) + step * 4
            rows = rows_out[pl.ds(at, 4)].reshape(-1, rows_out.shape[2])
            tokens = rows[:, :width]
            shares = rows[:, width:].astype(jnp.float32)
            lane = lax.broadcasted_iota(jnp.int32, shares.shape, 1)
            own = jnp.logical_or(lane == me, lane == me + count)
            own_mix = jnp.sum(jnp.where(own, shares, 0.0), axis=1, keepdims=True)
            gate = gate_out[...].reshape(width, -1)
            gate_proj = jnp.dot(tokens, gate, preferred_element_type=jnp.float32)
            up = up_out[...].reshape(width, -1)
            up_proj = jnp.dot(tokens, up, preferred_element_type=jnp.float32)
            hidden = gate_proj / (1.0 + jnp.exp(-gate_proj)) * up_proj * own_mix
            place = pl.ds(pl.multiple_of(at * rows_out.shape[1], rows.shape[0]), rows.shape[0])
            hidden_ref[place, :] = hidden.astype(hidden_ref.dtype)

    half = count // 2
    order = [r for i in range(half) for r in ((half + i, i) if i else (half,))]
    first = [(kind, r) for r in order for kind in ((0, 2) if r < NEAR else (0,))]
    items = first + [(1, r) for r in order]
    spacing = len(items) // (line + 1)
    side_at = 2 + spacing * (line - 1) + 3

    def advance(i):
        pass_on(*items[i])
        before_last = len(items) - 1 - i
        if before_last % 2 == 0 and before_last < 8:
            if before_last == 6:
                ready()
            expert_rows(3 - before_last // 2)

    for i, item in enumerate(items):
        start_weight(*item)
        if i >= 2 and (i - 2) % spacing == 0 and (i - 2) // spacing < line - 1:
            line_step((i - 2) // spacing)
        if i == side_at:
            for index in range(line):
                side_step(index)
        if i == AHEAD:
            for copy in own_copies:
                copy.start()
        if i >= AHEAD:
            advance(i - AHEAD)
    for i in range(len(items) - AHEAD, len(items)):
        advance(i)

    own_copies[2].wait()
    for kind, r in items:
        across(kind, r, ins, outs, 0).wait_send()
        for h in range(1, groups if r >= NEAR else 1):
            onward(kind, r, h, 0).wait_send()
            if kind == 1:
                onward(kind, r, h, 0).wait_recv()
    for index in range(line):
        block = lax.rem(me, 4) + 4 * index

        @pl.when(jnp.logical_and(has_up, index <= layer))
        def _():
            row_copy(0, block, me ^ 1).wait_send()

        @pl.when(jnp.logical_and(has_down, index >= layer))
        def _():
            row_copy(1, block, me ^ 1).wait_send()

        row_copy(2, block, me ^ 1).wait_send()
        row_copy(3, block, me ^ 1).wait_send()
        row_copy(3, block ^ 2, me ^ 1).wait_send()


def move(groups, gate_train, up_train, down_train, row_block):
    count = gate_train.shape[0]
    anywhere = pl.BlockSpec(memory_space=pl.ANY)
    DMA = pltpu.SemaphoreType.DMA
    return pl.pallas_call(
        functools.partial(move_kernel, groups, count),
        out_shape=[
            jax.ShapeDtypeStruct((count * row_block.shape[0], gate_train.shape[2]), jnp.bfloat16),
            jax.ShapeDtypeStruct(down_train.shape, down_train.dtype),
        ],
        in_specs=[anywhere, anywhere, anywhere, pl.BlockSpec(memory_space=pltpu.VMEM)],
        out_specs=[pl.BlockSpec(memory_space=pltpu.VMEM), anywhere],
        scratch_shapes=[
            pltpu.VMEM(gate_train.shape, gate_train.dtype),
            pltpu.VMEM(up_train.shape, up_train.dtype),
            pltpu.VMEM((count,) + row_block.shape, row_block.dtype),
            DMA((2, count)), DMA((2, count)),
            DMA((2, count, max(1, groups - 1))), DMA((2, count, max(1, groups - 1))),
            DMA((4,)), DMA((4, count)), DMA((count,)),
        ],
        compiler_params=pltpu.CompilerParams(collective_id=0, has_side_effects=True, vmem_limit_bytes=60 * 2**20),
    )(gate_train, up_train, down_train, row_block)


def sum_kernel(
    count, part_ref, out_ref, core_in, side_in, up_in, down_in, side_out, up_out, down_out,
    core_send, core_recv, side_send, side_recv, up_send, up_recv, down_send, down_recv,
):
    me = lax.axis_index("expert")
    group = lax.axis_index("groups")
    line, layer = count // 4, me // 4
    place = lax.rem(me, 4)
    side, core = place // 2, lax.rem(place, 2)
    has_up, has_down = me + 4 < count, me >= 4
    greet([
        (None, (group, me ^ 1)), (None, (group, me ^ 2)),
        (has_up, (group, me + 4)), (has_down, (group, me - 4)),
    ])
    chunk = 16
    row_count = part_ref.shape[1]

    def remote(src, dst, send, recv, target):
        return pltpu.make_async_remote_copy(
            src_ref=src, dst_ref=dst, send_sem=send, recv_sem=recv, device_id=(group, target), device_id_type=MESH
        )

    def add(target, *sources):
        @pl.loop(0, row_count // chunk)
        def _(step):
            rows = pl.ds(pl.multiple_of(step * chunk, chunk), chunk)
            total = sources[0][rows, :].astype(jnp.float32)
            for source in sources[1:]:
                total = total + source[rows, :].astype(jnp.float32)
            target[rows, :] = total.astype(target.dtype)

    def core_copy(at, y):
        slot = at * 2 + y
        return remote(
            part_ref.at[at * 4 + y * 2 + (core ^ 1)], core_in.at[slot], core_send.at[slot], core_recv.at[slot], me ^ 1
        )

    def side_copy(at):
        return remote(side_out.at[at], side_in.at[at], side_send.at[at], side_recv.at[at], me ^ 2)

    def up_copy(at):
        return remote(up_out.at[at], up_in.at[at], up_send.at[at], up_recv.at[at], me + 4)

    def down_copy(at):
        return remote(down_out.at[at], down_in.at[at], down_send.at[at], down_recv.at[at], me - 4)

    def in_order(act):
        for d in range(line - 1, 0, -1):
            pl.when(layer + d < line)(functools.partial(act, layer + d, 1))
            pl.when(layer - d >= 0)(functools.partial(act, layer - d, -1))
        act(layer, 0)

    in_order(lambda at, way: core_copy(at, side ^ 1).start())
    in_order(lambda at, way: core_copy(at, side).start())

    def to_side(at, way):
        core_copy(at, side ^ 1).wait_recv()
        add(side_out.at[at], part_ref.at[at * 4 + (side ^ 1) * 2 + core], core_in.at[at * 2 + (side ^ 1)])
        side_copy(at).start()

    in_order(to_side)

    def along(at, way):
        core_copy(at, side).wait_recv()
        side_copy(at).wait_recv()
        mine = (part_ref.at[at * 4 + place], core_in.at[at * 2 + side], side_in.at[at])
        if way == 1:
            @pl.when(has_down)
            def _():
                up_copy(at).wait_recv()
                add(up_out.at[at], *mine, up_in.at[at])

            @pl.when(jnp.logical_not(has_down))
            def _():
                add(up_out.at[at], *mine)

            up_copy(at).start()
        elif way == -1:
            @pl.when(has_up)
            def _():
                down_copy(at).wait_recv()
                add(down_out.at[at], *mine, down_in.at[at])

            @pl.when(jnp.logical_not(has_up))
            def _():
                add(down_out.at[at], *mine)

            down_copy(at).start()
        else:
            @pl.when(has_down)
            def _():
                up_copy(at).wait_recv()

            @pl.when(has_up)
            def _():
                down_copy(at).wait_recv()

            both = jnp.logical_and(has_down, has_up)

            @pl.when(both)
            def _():
                add(out_ref, *mine, up_in.at[at], down_in.at[at])

            @pl.when(jnp.logical_and(has_down, jnp.logical_not(has_up)))
            def _():
                add(out_ref, *mine, up_in.at[at])

            @pl.when(jnp.logical_and(has_up, jnp.logical_not(has_down)))
            def _():
                add(out_ref, *mine, down_in.at[at])

            @pl.when(jnp.logical_not(jnp.logical_or(has_up, has_down)))
            def _():
                add(out_ref, *mine)

    in_order(along)

    def finish(at, way):
        core_copy(at, side ^ 1).wait_send()
        core_copy(at, side).wait_send()
        side_copy(at).wait_send()
        if way == 1:
            up_copy(at).wait_send()
        if way == -1:
            down_copy(at).wait_send()

    in_order(finish)


def summed(partial_out, count):
    rows, width = partial_out.shape[0] // count, partial_out.shape[1]
    line = count // 4
    DMA = pltpu.SemaphoreType.DMA
    block = lambda amount: pltpu.VMEM((amount, rows, width), jnp.bfloat16)
    return pl.pallas_call(
        functools.partial(sum_kernel, count),
        out_shape=jax.ShapeDtypeStruct((rows, width), jnp.bfloat16),
        in_specs=[pl.BlockSpec(memory_space=pltpu.VMEM)],
        out_specs=pl.BlockSpec(memory_space=pltpu.VMEM),
        scratch_shapes=[block(count // 2)] + [block(line)] * 6
        + [DMA((count // 2,)), DMA((count // 2,))] + [DMA((line,))] * 6,
        compiler_params=pltpu.CompilerParams(collective_id=1, has_side_effects=True, vmem_limit_bytes=60 * 2**20),
    )(partial_out.reshape(count, rows, width))


def local(
    queries,
    key_cache,
    value_cache,
    new_key,
    new_value,
    cache_lengths,
    hidden_in,
    norm_gain,
    router_weight,
    expert_ids,
    gate_train,
    up_train,
    down_train,
):
    width = hidden_in.shape[1]
    expert_count = router_weight.shape[1]
    normed = rms_normed(hidden_in, norm_gain)
    mixing = dense_mixing(normed, router_weight, expert_ids)
    mixing_high = mixing.astype(jnp.bfloat16)
    mixing_low = (mixing - mixing_high.astype(jnp.float32)).astype(jnp.bfloat16)
    spare = -2 * expert_count % 128
    row_block = jnp.concatenate(
        [normed, mixing_high, mixing_low, jnp.zeros((normed.shape[0], spare), jnp.bfloat16)], axis=1
    )
    hidden_units, down_moved = move(
        lax.axis_size("groups"), gate_train, up_train, down_train, row_block
    )
    down_moved = down_moved.reshape(-1, width)
    attended = attend(queries, key_cache, value_cache, new_key, new_value, cache_lengths)
    partial_out = jnp.dot(hidden_units, down_moved, preferred_element_type=jnp.float32).astype(jnp.bfloat16)
    mixed_out = summed(partial_out, expert_count)
    return (attended, mixed_out)


def solution(mesh):
    placed = (
        P(("groups", "expert"), None),
        P(("groups", "expert"), None, None),
        P(("groups", "expert"), None, None),
        P(("groups", "expert"), None),
        P(("groups", "expert"), None),
        P(("groups", "expert")),
        P(("groups", "expert"), None),
        P(),
        P(),
        P(("groups", "expert"), None),
        P(None, "expert", None),
        P(None, "expert", None),
        P(None, "expert", None),
    )
    return jax.shard_map(
        local,
        mesh=mesh,
        in_specs=placed,
        out_specs=(P(("groups", "expert"), None), P(("groups", "expert"), None)),
        check_vma=False,
    )
```

profile of v0, /device:TPU:0, one launch (start us, length us, event | category | flops | bytes accessed | tf_op | source)
XLA Modules:
  0.0 192.4 jit_solution(14041173040760905776)
XLA Ops:
  0.6 0.0 copy-start
  0.6 0.7 convert_element_type.43
  1.4 1.1 fusion.3
  2.5 1.1 fusion.5
  3.6 0.7 fusion.13
  4.3 0.1 copy.31
  4.4 1.1 fusion.24
  5.6 0.2 fusion.18
  5.8 0.1 subtract_convert_fusion
  5.9 0.8 concatenate.3.rows_ref
  6.7 137.0 %shard_map.140 = (bf16[1024,768]{1,0:T(8,128)(2,1)}, bf16[16,48,2048]{2,1,0:T(8,128)(2,1)}) custom-call(bf16[16,128,768]{2,1,0:T(8,128)(2,1)} %gate_ref.1, bf16[16,128,768]{2,1,0:T(8,128)(2,1)} %up_ref.1, bf16[16,48,2048]{2,1,0:T(8,128)(2,1)} %down_ref.1, bf16[64,2176]{1,0:T(8,128)(2,1)} %concatenate.3.rows_ref), custom_call_target="tpu_custom_call" | custom-call | tf_op jit(solution)/shard_map/pallas_call | solution.py:313
  143.7 7.7 %convolution_convert_fusion = bf16[1024,2048]{1,0:T(8,128)(2,1)} fusion(bf16[1024,768]{1,0:T(8,128)(2,1)} %get-tuple-element.4, bf16[768,2048]{1,0:T(8,128)(2,1)} %bitcast.43), kind=kOutput, calls=%fused_computation | convolution fusion | flops 3223322624 | bytes 8912896 | tf_op jit(solution)/shard_map/dot_general | solution.py:508
  151.4 0.0 copy-start.5
  151.4 0.0 copy-start.1
  151.4 0.0 copy-start.2
  151.4 0.0 copy-start.4
  151.4 0.0 copy-start.3
  151.4 37.3 %shard_map.141 = bf16[64,2048]{1,0:T(8,128)(2,1)} custom-call(bf16[16,64,2048]{2,1,0:T(8,128)(2,1)} %bitcast.37), custom_call_target="tpu_custom_call" | custom-call | tf_op jit(solution)/shard_map/pallas_call | solution.py:467
  188.7 0.0 copy-done.5
  188.7 0.1 iota_compare_fusion.1
  188.8 0.0 copy-done.1
  188.8 0.0 copy-done.2
  188.8 0.5 fusion.23
  189.3 0.0 copy-done.4
  189.3 0.2 fusion.14
  189.5 0.2 fusion.10
  189.7 0.0 copy-done.3
  189.8 0.0 copy-done
  189.8 0.3 fusion.2
  190.1 0.7 copy.59
  190.8 1.7 copy.62
  (6 shorter events, 0.1 us)
Async XLA Ops:
  0.6 189.1 %copy-start = (bf16[8,64,512]{2,1,0:T(8,128)(2,1)S(1)}, bf16[8,64,512]{2,1,0:T(8,128)(2,1)}, u32[]{:S(2)}) copy-start(bf16[8,64,512]{2,1,0:T(8,128)(2,1)} %param.15) | copy-start | bytes 1572868
  151.4 37.4 %copy-start.5 = (s32[8]{0:T(128)S(1)}, s32[8]{0:T(128)}, u32[]{:S(2)}) copy-start(s32[8]{0:T(128)} %param.18) | copy-start | bytes 100
  151.4 37.4 %copy-start.1 = (bf16[8,64,512]{2,1,0:T(8,128)(2,1)S(1)}, bf16[8,64,512]{2,1,0:T(8,128)(2,1)}, u32[]{:S(2)}) copy-start(bf16[8,64,512]{2,1,0:T(8,128)(2,1)} %param.14) | copy-start | bytes 1572868
  151.4 37.4 %copy-start.2 = (bf16[8,4096]{1,0:T(8,128)(2,1)S(1)}, bf16[8,4096]{1,0:T(8,128)(2,1)}, u32[]{:S(2)}) copy-start(bf16[8,4096]{1,0:T(8,128)(2,1)} %param.13) | copy-start | bytes 196612
  151.4 37.9 %copy-start.4 = (bf16[8,512]{1,0:T(8,128)(2,1)S(1)}, bf16[8,512]{1,0:T(8,128)(2,1)}, u32[]{:S(2)}) copy-start(bf16[8,512]{1,0:T(8,128)(2,1)} %param.16) | copy-start | bytes 24580
  151.4 38.3 %copy-start.3 = (bf16[8,512]{1,0:T(8,128)(2,1)S(1)}, bf16[8,512]{1,0:T(8,128)(2,1)}, u32[]{:S(2)}) copy-start(bf16[8,512]{1,0:T(8,128)(2,1)} %param.17) | copy-start | bytes 24580
where the time goes:
time: 193 us; the launch traced here: 192 us
  Pallas kernels  174 us (90%)
  matrix products  9.81 us (5%)
  other arithmetic  4.27 us (2%)
  local copies, waits for them, and re-layouts  3.27 us (2%)
    pallas_call x1, Pallas kernels, move(): pl.pallas_call(functools.partial(move_kernel, groups, count), out_shape=[...  137 us
    pallas_call x1, Pallas kernels, summed(): pl.pallas_call(functools.partial(sum_kernel, count), out_shape=jax.ShapeD...  37.3 us
    dot_general x1, matrix products, local(): jnp.dot(hidden_units, down_moved, preferred_element_type=jnp.float32)  7.71 us

commit v1 on v0

--- a/solution.py
+++ b/solution.py
@@ -70,6 +70,7 @@
 MESH = pl.DeviceIdType.MESH
 AHEAD = 4
 NEAR = 4
+LAG = 2
 
 
 def greet(targets):
@@ -475,6 +476,305 @@
     )(partial_out.reshape(count, rows, width))
 
 
+def dims_fit(groups, count, gate_train, down_train, row_count):
+    rows, width = gate_train.shape[1], gate_train.shape[2]
+    part = down_train.shape[1]
+    return (
+        groups == 2
+        and count % 8 == 0
+        and 2 * count <= 128
+        and rows % 128 == 0
+        and part % 16 == 0
+        and part * count == width
+        and width % 256 == 0
+        and row_count % 16 == 0
+        and (count * row_count) % 512 == 0
+    )
+
+
+def hidden_kernel(
+    count, hid_ref, gain_ref, router_ref, ids_ref, gate_ref, up_ref,
+    hidden_ref, load, stage, wt, rows, acc,
+    load_sem, send_w, recv_w, send_x, recv_x, send_rows, recv_rows,
+):
+    me = lax.axis_index("expert")
+    group = lax.axis_index("groups")
+    other_group = 1 - group
+    line = count // 4
+    layer = me // 4
+    row_count, width = hid_ref.shape
+    depth = gate_ref.shape[1]
+    part = stage.shape[2] // count
+    total_f = stage.shape[2]
+    tokens = count * row_count
+
+    def loading(m, e):
+        return pltpu.make_async_copy((gate_ref, up_ref)[m].at[e], load.at[m, e], load_sem.at[m, e])
+
+    for e in range(count):
+        for m in range(2):
+            loading(m, e).start()
+
+    barrier = pltpu.get_barrier_semaphore()
+    peers = [(group, me ^ r) for r in range(1, count)] + [(other_group, me)]
+    for peer in peers:
+        pl.semaphore_signal(barrier, inc=1, device_id=peer, device_id_type=MESH)
+
+    values = hid_ref[...].astype(jnp.float32)
+    mean_square = jnp.mean(values * values, axis=-1, keepdims=True)
+    normed = (values * lax.rsqrt(mean_square + EPSILON) * gain_ref[...].astype(jnp.float32)).astype(jnp.bfloat16)
+    rows[me, :, :width] = normed
+    logits = jnp.dot(normed, router_ref[...], preferred_element_type=jnp.float32)
+    lane = lax.broadcasted_iota(jnp.int32, logits.shape, 1)
+    picked = ids_ref[:, 0:1] == lane
+    for k in range(1, ids_ref.shape[1]):
+        picked = jnp.logical_or(picked, ids_ref[:, k : k + 1] == lane)
+    masked = jnp.where(picked, logits, -jnp.inf)
+    raised = jnp.exp(masked - jnp.max(masked, axis=-1, keepdims=True))
+    mixing = raised / jnp.sum(raised, axis=-1, keepdims=True)
+    high = mixing.astype(jnp.bfloat16)
+    low = (mixing - high.astype(jnp.float32)).astype(jnp.bfloat16)
+    source = lax.broadcasted_iota(jnp.int32, (count, 128), 0)
+    place = lax.broadcasted_iota(jnp.int32, (count, 128), 1)
+    at_high = jnp.where(place == source, 1.0, 0.0).astype(jnp.bfloat16)
+    at_low = jnp.where(place == source + count, 1.0, 0.0).astype(jnp.bfloat16)
+    shares = jnp.dot(high, at_high, preferred_element_type=jnp.float32) + jnp.dot(
+        low, at_low, preferred_element_type=jnp.float32
+    )
+    rows[me, :, width:] = shares.astype(jnp.bfloat16)
+
+    pl.semaphore_wait(barrier, len(peers))
+
+    def remote(src, dst, send, recv, target):
+        return pltpu.make_async_remote_copy(
+            src_ref=src, dst_ref=dst, send_sem=send, recv_sem=recv, device_id=target, device_id_type=MESH
+        )
+
+    def row_copy(kind, block, target):
+        return remote(
+            rows.at[block], rows.at[block], send_rows.at[kind, block], recv_rows.at[block], (group, target)
+        )
+
+    def row_wait(block):
+        row_copy(0, block, me ^ 1).wait_recv()
+
+    has_up, has_down = me + 4 < count, me >= 4
+
+    @pl.when(has_up)
+    def _():
+        row_copy(0, me, me + 4).start()
+
+    @pl.when(has_down)
+    def _():
+        row_copy(1, me, me - 4).start()
+
+    row_copy(2, me, me ^ 2).start()
+    row_copy(3, me, me ^ 1).start()
+
+    def line_step(step):
+        below, above = me - 4 * (step + 1), me + 4 * (step + 1)
+
+        @pl.when(below >= 0)
+        def _():
+            row_wait(below)
+
+            @pl.when(has_up)
+            def _():
+                row_copy(0, below, me + 4).start()
+
+            row_copy(2, below, me ^ 2).start()
+            row_copy(3, below, me ^ 1).start()
+
+        @pl.when(above < count)
+        def _():
+            row_wait(above)
+
+            @pl.when(has_down)
+            def _():
+                row_copy(1, above, me - 4).start()
+
+            row_copy(2, above, me ^ 2).start()
+            row_copy(3, above, me ^ 1).start()
+
+    def side_step():
+        for index in range(line):
+            block = (lax.rem(me, 4) ^ 2) + 4 * index
+            row_wait(block)
+            row_copy(3, block, me ^ 1).start()
+
+    def rows_ready():
+        for index in range(line):
+            for y in range(2):
+                row_wait(4 * index + 2 * y + (lax.rem(me, 2) ^ 1))
+
+    def lanes_of(owner):
+        return pl.ds(pl.multiple_of(owner * depth, depth), depth)
+
+    def across(m, r):
+        target = me ^ r
+        index = m if r < NEAR else group
+        slot = m if r < NEAR else 0
+        return remote(
+            stage.at[index, target], wt.at[index, :, lanes_of(me)],
+            send_w.at[slot, r], recv_w.at[slot, r], (group, target),
+        )
+
+    def onward(r):
+        held = me ^ r
+        ref = wt.at[group, :, lanes_of(held)]
+        return remote(ref, ref, send_x.at[r], recv_x.at[r], (other_group, me))
+
+    def start_weight(r):
+        for m in range(2 if r < NEAR else 1):
+            across(m, r).start()
+
+    def pass_on(r):
+        for m in range(2 if r < NEAR else 1):
+            across(m, r).wait_recv()
+        if r >= NEAR:
+            onward(r).start()
+
+    @pl.loop(0, count)
+    def _(e):
+        for m in range(2):
+            loading(m, e).wait()
+            turned = load[m, e].T.reshape(count, part, depth)
+            stage[m, :, pl.ds(pl.multiple_of(e * part, part), part), :] = turned
+
+    for m in range(2):
+        wt[m, :, lanes_of(me)] = stage[m, me]
+
+    tile = 256
+    tiles = total_f // tile
+    chunk = 512
+    chunks = tokens // chunk
+    blocks = chunk // row_count
+
+    def accumulate(r, first):
+        for q in (r, r ^ 1):
+            if q >= NEAR:
+                onward(q).wait_recv()
+        base = pl.multiple_of(((me ^ r) // 2) * (2 * depth), 2 * depth)
+
+        @pl.loop(0, 2 * tiles)
+        def _(step):
+            m, n = step // tiles, step % tiles
+            weight = wt[m, pl.ds(pl.multiple_of(n * tile, tile), tile), pl.ds(base, 2 * depth)]
+
+            @pl.loop(0, chunks)
+            def _(c):
+                x = rows[pl.ds(c * blocks, blocks), :, pl.ds(base, 2 * depth)].reshape(chunk, 2 * depth)
+                product = lax.dot_general(
+                    x, weight, (((1,), (1,)), ((), ())), preferred_element_type=jnp.float32
+                )
+                at = pl.ds(pl.multiple_of(c * chunk, chunk), chunk)
+                if first:
+                    acc[step, at, :] = product
+                else:
+                    acc[step, at, :] = acc[step, at, :] + product
+
+    half = count // 2
+    order = [r for i in range(half) for r in ((half + i, i) if i else (half,))]
+    passed, pending, done = {0}, [], 0
+    side_at = 2 * line
+
+    def after(i):
+        nonlocal done
+        r = order[i]
+        pass_on(r)
+        passed.add(r)
+        if r ^ 1 in passed:
+            pending.append((i, r))
+
+    started_rows = False
+
+    def compute(i):
+        nonlocal done, started_rows
+        while pending and (pending[0][0] + LAG <= i):
+            _, r = pending.pop(0)
+            if not started_rows:
+                rows_ready()
+                started_rows = True
+            accumulate(r, done == 0)
+            done += 1
+
+    for i, r in enumerate(order):
+        start_weight(r)
+        if i % 2 == 1 and i // 2 < line - 1:
+            line_step(i // 2)
+        if i == side_at:
+            side_step()
+        if i >= AHEAD:
+            after(i - AHEAD)
+            if i > side_at:
+                compute(i - AHEAD)
+    for i in range(len(order) - AHEAD, len(order)):
+        after(i)
+        compute(i)
+    compute(len(order) + LAG)
+
+    spread_at = lax.broadcasted_iota(jnp.int32, (128, total_f), 0)
+    column = lax.broadcasted_iota(jnp.int32, (128, total_f), 1)
+    expert = jnp.where(spread_at < count, spread_at, spread_at - count)
+    inside = jnp.logical_and(column >= expert * part, column < expert * part + part)
+    spread = jnp.where(jnp.logical_and(inside, spread_at < 2 * count), 1.0, 0.0).astype(jnp.bfloat16)
+
+    @pl.loop(0, count)
+    def _(b):
+        mix = jnp.dot(rows[b, :, width:], spread, preferred_element_type=jnp.float32)
+        at = pl.ds(pl.multiple_of(b * row_count, row_count), row_count)
+        for n in range(tiles):
+            gate_proj = acc[n, at, :]
+            up_proj = acc[tiles + n, at, :]
+            columns = slice(n * tile, (n + 1) * tile)
+            hidden = gate_proj / (1.0 + jnp.exp(-gate_proj)) * up_proj * mix[:, columns]
+            hidden_ref[at, columns] = hidden.astype(hidden_ref.dtype)
+
+    for r in order:
+        for m in range(2 if r < NEAR else 1):
+            across(m, r).wait_send()
+        if r >= NEAR:
+            onward(r).wait_send()
+    for index in range(line):
+        block = lax.rem(me, 4) + 4 * index
+
+        @pl.when(jnp.logical_and(has_up, index <= layer))
+        def _():
+            row_copy(0, block, me ^ 1).wait_send()
+
+        @pl.when(jnp.logical_and(has_down, index >= layer))
+        def _():
+            row_copy(1, block, me ^ 1).wait_send()
+
+        row_copy(2, block, me ^ 1).wait_send()
+        row_copy(3, block, me ^ 1).wait_send()
+        row_copy(3, block ^ 2, me ^ 1).wait_send()
+
+
+def hidden_units_of(hidden_in, norm_gain, router_weight, expert_ids, gate_train, up_train):
+    count, depth, total_f = gate_train.shape
+    row_count, width = hidden_in.shape
+    anywhere = pl.BlockSpec(memory_space=pl.ANY)
+    near = pl.BlockSpec(memory_space=pltpu.VMEM)
+    DMA = pltpu.SemaphoreType.DMA
+    return pl.pallas_call(
+        functools.partial(hidden_kernel, count),
+        out_shape=jax.ShapeDtypeStruct((count * row_count, total_f), jnp.bfloat16),
+        in_specs=[near, near, near, near, anywhere, anywhere],
+        out_specs=near,
+        scratch_shapes=[
+            pltpu.VMEM((2, count, depth, total_f), jnp.bfloat16),
+            pltpu.VMEM((2, count, total_f, depth), jnp.bfloat16),
+            pltpu.VMEM((2, total_f, count * depth), jnp.bfloat16),
+            pltpu.VMEM((count, row_count, width + 128), jnp.bfloat16),
+            pltpu.VMEM((2 * total_f // 256, count * row_count, 256), jnp.float32),
+            DMA((2, count)), DMA((2, count)), DMA((2, count)), DMA((count,)), DMA((count,)),
+            DMA((4, count)), DMA((count,)),
+        ],
+        compiler_params=pltpu.CompilerParams(collective_id=2, has_side_effects=True, vmem_limit_bytes=60 * 2**20),
+    )(hidden_in, norm_gain.reshape(1, width), router_weight, expert_ids, gate_train, up_train)
+
+
 def local(
     queries,
     key_cache,
@@ -492,17 +792,20 @@
 ):
     width = hidden_in.shape[1]
     expert_count = router_weight.shape[1]
-    normed = rms_normed(hidden_in, norm_gain)
-    mixing = dense_mixing(normed, router_weight, expert_ids)
-    mixing_high = mixing.astype(jnp.bfloat16)
-    mixing_low = (mixing - mixing_high.astype(jnp.float32)).astype(jnp.bfloat16)
-    spare = -2 * expert_count % 128
-    row_block = jnp.concatenate(
-        [normed, mixing_high, mixing_low, jnp.zeros((normed.shape[0], spare), jnp.bfloat16)], axis=1
-    )
-    hidden_units, down_moved = move(
-        lax.axis_size("groups"), gate_train, up_train, down_train, row_block
-    )
+    groups = lax.axis_size("groups")
+    if dims_fit(groups, expert_count, gate_train, down_train, hidden_in.shape[0]):
+        hidden_units = hidden_units_of(hidden_in, norm_gain, router_weight, expert_ids, gate_train, up_train)
+        down_moved = down_train
+    else:
+        normed = rms_normed(hidden_in, norm_gain)
+        mixing = dense_mixing(normed, router_weight, expert_ids)
+        mixing_high = mixing.astype(jnp.bfloat16)
+        mixing_low = (mixing - mixing_high.astype(jnp.float32)).astype(jnp.bfloat16)
+        spare = -2 * expert_count % 128
+        row_block = jnp.concatenate(
+            [normed, mixing_high, mixing_low, jnp.zeros((normed.shape[0], spare), jnp.bfloat16)], axis=1
+        )
+        hidden_units, down_moved = move(groups, gate_train, up_train, down_train, row_block)
     down_moved = down_moved.reshape(-1, width)
     attended = attend(queries, key_cache, value_cache, new_key, new_value, cache_lengths)
     partial_out = jnp.dot(hidden_units, down_moved, preferred_element_type=jnp.float32).astype(jnp.bfloat16)

time: 193 us -> 176 us (0.912)
  Pallas kernels: 174 us -> 155 us
  local copies, waits for them, and re-layouts: 3.27 us -> 8.73 us
  other arithmetic: 4.27 us -> 1.69 us
    pallas_call x1, Pallas kernels: 137 us -> 121 us  [hidden_units_of(): pl.pallas_call(functools.partial(hidden_kernel, count), out_shape=jax.Sha...]
    unnamed x14 -> x6, local copies, waits for them, and re-layouts: 2.36 us -> 7.44 us
    pallas_call x1, Pallas kernels: 37.3 us -> 34 us  [summed(): pl.pallas_call(functools.partial(sum_kernel, count), out_shape=jax.ShapeD...]
    convert_element_type x3 -> x0, other arithmetic: 1.94 us -> none  [the longest x1 1.09 us: rms_normed(): (values * lax.rsqrt(mean_square + EPSILON) * norm_gain.astype(jnp.float32...]
where the time goes in v1:
time: 176 us
  Pallas kernels  155 us (88%)
  matrix products  10.3 us (6%)
  local copies, waits for them, and re-layouts  8.73 us (5%)
    pallas_call x1, Pallas kernels, hidden_units_of(): pl.pallas_call(functools.partial(hidden_kernel, count), out_shape=jax.Sha...  121 us
    pallas_call x1, Pallas kernels, summed(): pl.pallas_call(functools.partial(sum_kernel, count), out_shape=jax.ShapeD...  34 us
    unnamed x6, local copies, waits for them, and re-layouts  7.44 us
    dot_general x1, matrix products, local(): jnp.dot(hidden_units, down_moved, preferred_element_type=jnp.float32)  6.38 us

profile of v1, /device:TPU:0, one launch (start us, length us, event | category | flops | bytes accessed | tf_op | source)
XLA Modules:
  0.0 175.9 jit_solution(16689398613138149630)
XLA Ops:
  0.6 0.0 copy-start
  0.6 1.9 %copy-done = bf16[16,48,2048]{2,1,0:T(8,128)(2,1)S(1)} copy-done((bf16[16,48,2048]{2,1,0:T(8,128)(2,1)S(1)}, bf16[16,48,2048]{2,1,0:T(8,128)(2,1)}, u32[]{:S(2)}) %copy-start) | copy-done | bytes 3145752
  2.5 0.7 iota_compare_fusion
  3.3 1.3 reshape.52.gain_ref
  4.5 1.0 fusion.10
  5.5 0.7 bitcast_convert_fusion
  6.2 1.4 copy.20.ids_ref
  7.6 1.5 fusion.16
  9.2 0.2 fusion.7
  9.4 1.4 fusion.2
  10.8 0.7 copy.45
  11.5 1.8 %copy.19.router_ref = bf16[2048,16]{1,0:T(8,128)(2,1)} copy(bf16[2048,16]{0,1:T(8,128)(2,1)} %param.21) | data formatting | bytes 131072 | tf_op args[8]
  13.3 120.5 %shard_map.140 = bf16[1024,768]{1,0:T(8,128)(2,1)} custom-call(bf16[64,2048]{1,0:T(8,128)(2,1)} %hid_ref.1, bf16[1,2048]{1,0:T(2,128)(2,1)} %reshape.52.gain_ref, bf16[2048,16]{1,0:T(8,128)(2,1)} %copy.19.router_ref, s32[64,8]{1,0:T(8,128)} %copy.20.ids_ref, bf16[16,128,768]{2,1,0:T(8,128)(2,1)} %gate_ref.1, bf16[16,128,768]{2,1,0:T(8,128)(2,1)} %up_ref.1), custom_call_target="tpu_custom_call" | custom-call | tf_op jit(solution)/shard_map/pallas_call | solution.py:760
  133.9 6.4 %convolution_convert_fusion = bf16[1024,2048]{1,0:T(8,128)(2,1)} fusion(bf16[1024,768]{1,0:T(8,128)(2,1)} %shard_map.140, bf16[768,2048]{1,0:T(8,128)(2,1)S(1)} %bitcast.35), kind=kOutput, calls=%fused_computation | convolution fusion | flops 3223322624 | bytes 8912896 | tf_op jit(solution)/shard_map/dot_general | solution.py:811
  140.2 34.0 %shard_map.141 = bf16[64,2048]{1,0:T(8,128)(2,1)} custom-call(bf16[16,64,2048]{2,1,0:T(8,128)(2,1)} %bitcast.36), custom_call_target="tpu_custom_call" | custom-call | tf_op jit(solution)/shard_map/pallas_call | solution.py:468
  174.2 1.7 copy.47
  (3 shorter events, 0.0 us)
Async XLA Ops:
  0.6 1.9 %copy-start = (bf16[16,48,2048]{2,1,0:T(8,128)(2,1)S(1)}, bf16[16,48,2048]{2,1,0:T(8,128)(2,1)}, u32[]{:S(2)}) copy-start(bf16[16,48,2048]{2,1,0:T(8,128)(2,1)} %param.25) | copy-start | bytes 9437188

commit v2 on v1

--- a/solution.py
+++ b/solution.py
@@ -492,10 +492,16 @@
     )
 
 
-def hidden_kernel(
-    count, hid_ref, gain_ref, router_ref, ids_ref, gate_ref, up_ref,
-    hidden_ref, load, stage, wt, rows, acc,
-    load_sem, send_w, recv_w, send_x, recv_x, send_rows, recv_rows,
+def fused_kernel(
+    count, first_columns, lengths_ref, queries_ref, keys_ref, values_ref, new_key_ref, new_value_ref,
+    hidden_in_ref, gain_in_ref, router_in_ref, ids_in_ref, gate_ref, up_ref, down_in_ref,
+    attended_ref, out_ref,
+    queries, keys, cached, new_key, new_value, hid_ref, gain_ref, router_ref, ids_ref, down,
+    load, stage, wt, rows, acc, units, part, core_in, side_out, side_in,
+    early_up_out, early_up_in, early_down_out, early_down_in,
+    late_up_out, late_up_in, late_down_out, late_down_in, last_out, last_in,
+    small_sem, load_sem, send_w, recv_w, send_x, recv_x, send_rows, recv_rows,
+    core_send, core_recv, line_send, line_recv, last_send, last_recv,
 ):
     me = lax.axis_index("expert")
     group = lax.axis_index("groups")
@@ -504,31 +510,54 @@
     layer = me // 4
     row_count, width = hid_ref.shape
     depth = gate_ref.shape[1]
-    part = stage.shape[2] // count
+    share = stage.shape[2] // count
     total_f = stage.shape[2]
     tokens = count * row_count
 
     def loading(m, e):
         return pltpu.make_async_copy((gate_ref, up_ref)[m].at[e], load.at[m, e], load_sem.at[m, e])
 
+    small = [
+        pltpu.make_async_copy(src, dst, small_sem.at[i])
+        for i, (src, dst) in enumerate((
+            (hidden_in_ref, hid_ref), (gain_in_ref, gain_ref), (router_in_ref, router_ref), (ids_in_ref, ids_ref),
+            (queries_ref, queries), (keys_ref, keys), (values_ref, cached), (new_key_ref, new_key),
+            (new_value_ref, new_value), (down_in_ref, down),
+        ))
+    ]
+    for copy in small[:4]:
+        copy.start()
     for e in range(count):
         for m in range(2):
             loading(m, e).start()
+    for copy in small[4:]:
+        copy.start()
 
     barrier = pltpu.get_barrier_semaphore()
     peers = [(group, me ^ r) for r in range(1, count)] + [(other_group, me)]
     for peer in peers:
         pl.semaphore_signal(barrier, inc=1, device_id=peer, device_id_type=MESH)
 
+    for copy in small[:4]:
+        copy.wait()
     values = hid_ref[...].astype(jnp.float32)
     mean_square = jnp.mean(values * values, axis=-1, keepdims=True)
-    normed = (values * lax.rsqrt(mean_square + EPSILON) * gain_ref[...].astype(jnp.float32)).astype(jnp.bfloat16)
+    gain = gain_ref[...].astype(jnp.float32).reshape(1, width)
+    normed = (values * lax.rsqrt(mean_square + EPSILON) * gain).astype(jnp.bfloat16)
     rows[me, :, :width] = normed
-    logits = jnp.dot(normed, router_ref[...], preferred_element_type=jnp.float32)
-    lane = lax.broadcasted_iota(jnp.int32, logits.shape, 1)
-    picked = ids_ref[:, 0:1] == lane
-    for k in range(1, ids_ref.shape[1]):
-        picked = jnp.logical_or(picked, ids_ref[:, k : k + 1] == lane)
+    by_last = (((1,), (1,)), ((), ()))
+    logits = lax.dot_general(normed, router_ref[...], by_last, preferred_element_type=jnp.float32)
+    ids = ids_ref[...]
+    lane = lax.broadcasted_iota(jnp.int32, (count, row_count), 0)
+    named = ids[0:1, :] == lane
+    for k in range(1, ids.shape[0]):
+        named = jnp.logical_or(named, ids[k : k + 1, :] == lane)
+    named = jnp.where(named, 1.0, 0.0).astype(jnp.bfloat16)
+    diagonal = lax.broadcasted_iota(jnp.int32, (row_count, row_count), 0) == lax.broadcasted_iota(
+        jnp.int32, (row_count, row_count), 1
+    )
+    diagonal = jnp.where(diagonal, 1.0, 0.0).astype(jnp.bfloat16)
+    picked = lax.dot_general(diagonal, named, by_last, preferred_element_type=jnp.float32) > 0.5
     masked = jnp.where(picked, logits, -jnp.inf)
     raised = jnp.exp(masked - jnp.max(masked, axis=-1, keepdims=True))
     mixing = raised / jnp.sum(raised, axis=-1, keepdims=True)
@@ -638,8 +667,8 @@
     def _(e):
         for m in range(2):
             loading(m, e).wait()
-            turned = load[m, e].T.reshape(count, part, depth)
-            stage[m, :, pl.ds(pl.multiple_of(e * part, part), part), :] = turned
+            turned = load[m, e].T.reshape(count, share, depth)
+            stage[m, :, pl.ds(pl.multiple_of(e * share, share), share), :] = turned
 
     for m in range(2):
         wt[m, :, lanes_of(me)] = stage[m, me]
@@ -665,13 +694,55 @@
             def _(c):
                 x = rows[pl.ds(c * blocks, blocks), :, pl.ds(base, 2 * depth)].reshape(chunk, 2 * depth)
                 product = lax.dot_general(
-                    x, weight, (((1,), (1,)), ((), ())), preferred_element_type=jnp.float32
+                    x, weight, by_last, preferred_element_type=jnp.float32
                 )
                 at = pl.ds(pl.multiple_of(c * chunk, chunk), chunk)
                 if first:
                     acc[step, at, :] = product
                 else:
                     acc[step, at, :] = acc[step, at, :] + product
+
+    def attend_here():
+        for copy in small[4:9]:
+            copy.wait()
+        seq_count = queries.shape[0]
+        group_size = HEADS // KV_HEADS
+        shape = (group_size * seq_count, 1)
+        seq = jnp.bitwise_and(lax.broadcasted_iota(jnp.int32, shape, 0), seq_count - 1)
+        lengths = jnp.zeros(shape, jnp.int32)
+        for s in range(seq_count):
+            lengths = jnp.where(seq == s, lengths_ref[s], lengths)
+        span = seq_count * CTX
+        position = lax.broadcasted_iota(jnp.int32, (shape[0], span), 1) - seq * CTX
+        visible = jnp.logical_and(position >= 0, position < lengths)
+        score_scale = 1.0 / math.sqrt(HEAD_DIM)
+
+        def columns_of(index):
+            return slice(index * HEAD_DIM, (index + 1) * HEAD_DIM)
+
+        for g in range(KV_HEADS):
+            mine = [queries[:, columns_of(g * group_size + h)].astype(jnp.float32) for h in range(group_size)]
+            asked = jnp.concatenate(mine, axis=0)
+            key = keys[:, :, columns_of(g)].reshape(span, HEAD_DIM)
+            value = cached[:, :, columns_of(g)].reshape(span, HEAD_DIM)
+            fresh_key = jnp.concatenate([new_key[:, columns_of(g)].astype(jnp.float32)] * group_size, axis=0)
+            fresh_value = jnp.concatenate([new_value[:, columns_of(g)].astype(jnp.float32)] * group_size, axis=0)
+            scores = score_scale * lax.dot_general(
+                asked.astype(jnp.bfloat16), key, by_last, preferred_element_type=jnp.float32
+            )
+            scores = jnp.where(visible, scores, -1e30)
+            own_score = jnp.sum(asked * fresh_key, axis=-1, keepdims=True) * score_scale
+            largest = jnp.maximum(jnp.max(scores, axis=-1, keepdims=True), own_score)
+            cached_exp = jnp.exp(scores - largest)
+            own_exp = jnp.exp(own_score - largest)
+            prob_total = jnp.sum(cached_exp, axis=-1, keepdims=True) + own_exp
+            cached_prob = (cached_exp / prob_total).astype(jnp.bfloat16)
+            own_prob = (own_exp / prob_total).astype(jnp.bfloat16).astype(jnp.float32)
+            context = jnp.dot(cached_prob, value, preferred_element_type=jnp.float32) + own_prob * fresh_value
+            for h in range(group_size):
+                attended_ref[:, columns_of(g * group_size + h)] = context[
+                    h * seq_count : (h + 1) * seq_count, :
+                ].astype(attended_ref.dtype)
 
     half = count // 2
     order = [r for i in range(half) for r in ((half + i, i) if i else (half,))]
@@ -704,6 +775,8 @@
             line_step(i // 2)
         if i == side_at:
             side_step()
+        if i == AHEAD - 1:
+            attend_here()
         if i >= AHEAD:
             after(i - AHEAD)
             if i > side_at:
@@ -716,20 +789,165 @@
     spread_at = lax.broadcasted_iota(jnp.int32, (128, total_f), 0)
     column = lax.broadcasted_iota(jnp.int32, (128, total_f), 1)
     expert = jnp.where(spread_at < count, spread_at, spread_at - count)
-    inside = jnp.logical_and(column >= expert * part, column < expert * part + part)
+    inside = jnp.logical_and(column >= expert * share, column < expert * share + share)
     spread = jnp.where(jnp.logical_and(inside, spread_at < 2 * count), 1.0, 0.0).astype(jnp.bfloat16)
 
-    @pl.loop(0, count)
-    def _(b):
-        mix = jnp.dot(rows[b, :, width:], spread, preferred_element_type=jnp.float32)
-        at = pl.ds(pl.multiple_of(b * row_count, row_count), row_count)
-        for n in range(tiles):
-            gate_proj = acc[n, at, :]
-            up_proj = acc[tiles + n, at, :]
-            columns = slice(n * tile, (n + 1) * tile)
-            hidden = gate_proj / (1.0 + jnp.exp(-gate_proj)) * up_proj * mix[:, columns]
-            hidden_ref[at, columns] = hidden.astype(hidden_ref.dtype)
-
+    place_in_layer = lax.rem(me, 4)
+    side, core = place_in_layer // 2, lax.rem(place_in_layer, 2)
+    first, second = pl.ds(0, first_columns), pl.ds(first_columns, width - first_columns)
+    small[9].wait()
+    table = []
+    for own in range(line):
+        seen = []
+        for d in range(line - 1, 0, -1):
+            seen += [own + d] * (own + d < line) + [own - d] * (own - d >= 0)
+        table.append(seen + [own])
+
+    def turn(j):
+        at = jnp.int32(0)
+        for own in range(line):
+            at = at + (layer == own).astype(jnp.int32) * table[own][j]
+        return at
+
+    def make_part(at):
+        @pl.loop(0, 4)
+        def _(b):
+            block = at * 4 + b
+            mix = jnp.dot(rows[block, :, width:], spread, preferred_element_type=jnp.float32)
+            here = pl.ds(pl.multiple_of(block * row_count, row_count), row_count)
+            there = pl.ds(pl.multiple_of(b * row_count, row_count), row_count)
+            for n in range(tiles):
+                gate_proj = acc[n, here, :]
+                up_proj = acc[tiles + n, here, :]
+                columns = slice(n * tile, (n + 1) * tile)
+                hidden = gate_proj / (1.0 + jnp.exp(-gate_proj)) * up_proj * mix[:, columns]
+                units[there, columns] = hidden.astype(units.dtype)
+
+        @pl.loop(0, width // tile)
+        def _(n):
+            columns = pl.ds(pl.multiple_of(n * tile, tile), tile)
+            product = jnp.dot(units[...], down[:, columns], preferred_element_type=jnp.float32)
+            part[pl.ds(at * 4, 4), :, columns] = product.astype(part.dtype).reshape(4, row_count, tile)
+
+    def add(target, *sources):
+        @pl.loop(0, row_count // 16)
+        def _(step):
+            here = pl.ds(pl.multiple_of(step * 16, 16), 16)
+            total = sources[0][here, :].astype(jnp.float32)
+            for source in sources[1:]:
+                total = total + source[here, :].astype(jnp.float32)
+            target[here, :] = total.astype(target.dtype)
+
+    def core_copy(at, y):
+        slot = at * 2 + y
+        return remote(
+            part.at[at * 4 + y * 2 + (core ^ 1)], core_in.at[slot], core_send.at[slot], core_recv.at[slot], (group, me ^ 1)
+        )
+
+    def line_copy(kind, at):
+        src, dst, target = (
+            (side_out, side_in, me ^ 2),
+            (early_up_out, early_up_in, me + 4),
+            (early_down_out, early_down_in, me - 4),
+            (late_up_out, late_up_in, me + 4),
+            (late_down_out, late_down_in, me - 4),
+        )[kind]
+        return remote(src.at[at], dst.at[at], line_send.at[kind, at], line_recv.at[kind, at], (group, target))
+
+    def last_copy():
+        return remote(last_out, last_in, last_send.at[0], last_recv.at[0], (group, me ^ 2))
+
+    def held(at, y, columns):
+        return part.at[at * 4 + y * 2 + core, :, columns], core_in.at[at * 2 + y, :, columns]
+
+    def to_side(at):
+        for y in range(2):
+            core_copy(at, y).wait_recv()
+        add(side_out.at[at], *held(at, side ^ 1, first))
+        line_copy(0, at).start()
+
+    def step_along(at, kinds, sources):
+        for kind, has_source, moving in ((kinds[0], has_down, at > layer), (kinds[1], has_up, at < layer)):
+            @pl.when(jnp.logical_and(moving, has_source))
+            def _():
+                line_copy(kind, at).wait_recv()
+                sources(kind, True)
+                line_copy(kind, at).start()
+
+            @pl.when(jnp.logical_and(moving, jnp.logical_not(has_source)))
+            def _():
+                sources(kind, False)
+                line_copy(kind, at).start()
+
+    def early(at):
+        def sources(kind, arriving):
+            out, arrived = ((early_up_out, early_up_in), (early_down_out, early_down_in))[kind - 1]
+            for y in range(2):
+                more = (arrived.at[at, y],) if arriving else ()
+                add(out.at[at, y], *held(at, y, second), *more)
+
+        step_along(at, (1, 2), sources)
+
+    def late(at):
+        line_copy(0, at).wait_recv()
+
+        def sources(kind, arriving):
+            out, arrived = ((late_up_out, late_up_in), (late_down_out, late_down_in))[kind - 3]
+            more = (arrived.at[at],) if arriving else ()
+            add(out.at[at], *held(at, side, first), side_in.at[at], *more)
+
+        step_along(at, (3, 4), sources)
+
+    def arrived_from(kinds, act):
+        @pl.when(has_down)
+        def _():
+            line_copy(kinds[0], layer).wait_recv()
+
+        @pl.when(has_up)
+        def _():
+            line_copy(kinds[1], layer).wait_recv()
+
+        for down_too, up_too in ((True, True), (True, False), (False, True)):
+            matches = jnp.logical_and(has_down == down_too, has_up == up_too)
+            pl.when(matches)(functools.partial(act, down_too, up_too))
+
+    for j in range(line):
+        at = turn(j)
+        make_part(at)
+        core_copy(at, side ^ 1).start()
+        core_copy(at, side).start()
+        if j:
+            to_side(turn(j - 1))
+    to_side(turn(line - 1))
+    for j in range(line - 1):
+        early(turn(j))
+    for j in range(line - 1):
+        late(turn(j))
+    line_copy(0, layer).wait_recv()
+
+    def sum_early(down_too, up_too):
+        for y, target in ((side ^ 1, last_out), (side, out_ref.at[:, second])):
+            more = [ref.at[layer, y] for ref, on in ((early_up_in, down_too), (early_down_in, up_too)) if on]
+            add(target, *held(layer, y, second), *more)
+
+    def sum_late(down_too, up_too):
+        more = [ref.at[layer] for ref, on in ((late_up_in, down_too), (late_down_in, up_too)) if on]
+        add(out_ref.at[:, first], *held(layer, side, first), side_in.at[layer], *more)
+
+    arrived_from((1, 2), sum_early)
+    last_copy().start()
+    arrived_from((3, 4), sum_late)
+    last_copy().wait_recv()
+    add(out_ref.at[:, second], out_ref.at[:, second], last_in)
+
+    last_copy().wait_send()
+    for at in range(line):
+        for y in range(2):
+            core_copy(at, y).wait_send()
+        line_copy(0, at).wait_send()
+        for up_kind in (1, 3):
+            pl.when(at > layer)(line_copy(up_kind, at).wait_send)
+            pl.when(at < layer)(line_copy(up_kind + 1, at).wait_send)
     for r in order:
         for m in range(2 if r < NEAR else 1):
             across(m, r).wait_send()
@@ -751,28 +969,54 @@
         row_copy(3, block ^ 2, me ^ 1).wait_send()
 
 
-def hidden_units_of(hidden_in, norm_gain, router_weight, expert_ids, gate_train, up_train):
+def fused(
+    queries, key_cache, value_cache, new_key, new_value, cache_lengths,
+    hidden_in, norm_gain, router_weight, expert_ids, gate_train, up_train, down_train,
+):
     count, depth, total_f = gate_train.shape
     row_count, width = hidden_in.shape
+    line = count // 4
+    first_columns = pl.cdiv(width * 6, 10 * 128) * 128
+    second_columns = width - first_columns
     anywhere = pl.BlockSpec(memory_space=pl.ANY)
     near = pl.BlockSpec(memory_space=pltpu.VMEM)
     DMA = pltpu.SemaphoreType.DMA
+    like = lambda x: pltpu.VMEM(x.shape, x.dtype)
+    held = lambda *shape: pltpu.VMEM(shape, jnp.bfloat16)
+    router_turned, ids_turned = router_weight.T, expert_ids.T
+    down_rows = down_train.reshape(-1, width)
     return pl.pallas_call(
-        functools.partial(hidden_kernel, count),
-        out_shape=jax.ShapeDtypeStruct((count * row_count, total_f), jnp.bfloat16),
-        in_specs=[near, near, near, near, anywhere, anywhere],
-        out_specs=near,
+        functools.partial(fused_kernel, count, first_columns),
+        out_shape=[
+            jax.ShapeDtypeStruct(queries.shape, jnp.bfloat16),
+            jax.ShapeDtypeStruct((row_count, width), jnp.bfloat16),
+        ],
+        in_specs=[pl.BlockSpec(memory_space=pltpu.SMEM)] + [anywhere] * 12,
+        out_specs=[near, near],
         scratch_shapes=[
-            pltpu.VMEM((2, count, depth, total_f), jnp.bfloat16),
-            pltpu.VMEM((2, count, total_f, depth), jnp.bfloat16),
-            pltpu.VMEM((2, total_f, count * depth), jnp.bfloat16),
-            pltpu.VMEM((count, row_count, width + 128), jnp.bfloat16),
+            like(queries), like(key_cache), like(value_cache), like(new_key), like(new_value),
+            like(hidden_in), like(norm_gain), like(router_turned), like(ids_turned), like(down_rows),
+            held(2, count, depth, total_f),
+            held(2, count, total_f, depth),
+            held(2, total_f, count * depth),
+            held(count, row_count, width + 128),
             pltpu.VMEM((2 * total_f // 256, count * row_count, 256), jnp.float32),
-            DMA((2, count)), DMA((2, count)), DMA((2, count)), DMA((count,)), DMA((count,)),
+            held(4 * row_count, total_f),
+            held(count, row_count, width),
+            held(2 * line, row_count, width),
+            held(line, row_count, first_columns), held(line, row_count, first_columns),
+            *[held(line, 2, row_count, second_columns)] * 4,
+            *[held(line, row_count, first_columns)] * 4,
+            held(row_count, second_columns), held(row_count, second_columns),
+            DMA((10,)), DMA((2, count)), DMA((2, count)), DMA((2, count)), DMA((count,)), DMA((count,)),
             DMA((4, count)), DMA((count,)),
+            DMA((2 * line,)), DMA((2 * line,)), DMA((5, line)), DMA((5, line)), DMA((1,)), DMA((1,)),
         ],
-        compiler_params=pltpu.CompilerParams(collective_id=2, has_side_effects=True, vmem_limit_bytes=60 * 2**20),
-    )(hidden_in, norm_gain.reshape(1, width), router_weight, expert_ids, gate_train, up_train)
+        compiler_params=pltpu.CompilerParams(collective_id=2, has_side_effects=True, vmem_limit_bytes=63 * 2**20),
+    )(
+        cache_lengths, queries, key_cache, value_cache, new_key, new_value,
+        hidden_in, norm_gain, router_turned, ids_turned, gate_train, up_train, down_rows,
+    )
 
 
 def local(
@@ -793,19 +1037,20 @@
     width = hidden_in.shape[1]
     expert_count = router_weight.shape[1]
     groups = lax.axis_size("groups")
-    if dims_fit(groups, expert_count, gate_train, down_train, hidden_in.shape[0]):
-        hidden_units = hidden_units_of(hidden_in, norm_gain, router_weight, expert_ids, gate_train, up_train)
-        down_moved = down_train
-    else:
-        normed = rms_normed(hidden_in, norm_gain)
-        mixing = dense_mixing(normed, router_weight, expert_ids)
-        mixing_high = mixing.astype(jnp.bfloat16)
-        mixing_low = (mixing - mixing_high.astype(jnp.float32)).astype(jnp.bfloat16)
-        spare = -2 * expert_count % 128
-        row_block = jnp.concatenate(
-            [normed, mixing_high, mixing_low, jnp.zeros((normed.shape[0], spare), jnp.bfloat16)], axis=1
-        )
-        hidden_units, down_moved = move(groups, gate_train, up_train, down_train, row_block)
+    if dims_fit(groups, expert_count, gate_train, down_train, hidden_in.shape[0]) and queries.shape[0] == 8:
+        return tuple(fused(
+            queries, key_cache, value_cache, new_key, new_value, cache_lengths,
+            hidden_in, norm_gain, router_weight, expert_ids, gate_train, up_train, down_train,
+        ))
+    normed = rms_normed(hidden_in, norm_gain)
+    mixing = dense_mixing(normed, router_weight, expert_ids)
+    mixing_high = mixing.astype(jnp.bfloat16)
+    mixing_low = (mixing - mixing_high.astype(jnp.float32)).astype(jnp.bfloat16)
+    spare = -2 * expert_count % 128
+    row_block = jnp.concatenate(
+        [normed, mixing_high, mixing_low, jnp.zeros((normed.shape[0], spare), jnp.bfloat16)], axis=1
+    )
+    hidden_units, down_moved = move(groups, gate_train, up_train, down_train, row_block)
     down_moved = down_moved.reshape(-1, width)
     attended = attend(queries, key_cache, value_cache, new_key, new_value, cache_lengths)
     partial_out = jnp.dot(hidden_units, down_moved, preferred_element_type=jnp.float32).astype(jnp.bfloat16)

time: 176 us -> 164 us (0.932)
  matrix products: 10.3 us -> 0 us
  local copies, waits for them, and re-layouts: 8.73 us -> 3.14 us
  Pallas kernels: 155 us -> 160 us
    dot_general x4 -> x0, matrix products: 10.3 us -> none  [the longest x1 6.38 us: local(): jnp.dot(hidden_units, down_moved, preferred_element_type=jnp.float32)]
    pallas_call x2 -> x1, Pallas kernels: 155 us -> 160 us  [fused(): pl.pallas_call(functools.partial(fused_kernel, count, first_columns), out...]
    unnamed x6 -> x2, local copies, waits for them, and re-layouts: 7.44 us -> 3.14 us
where the time goes in v2:
time: 164 us
  Pallas kernels  160 us (98%)
  local copies, waits for them, and re-layouts  3.14 us (2%)
    pallas_call x1, Pallas kernels, fused(): pl.pallas_call(functools.partial(fused_kernel, count, first_columns), out...  160 us

profile of v2, /device:TPU:0, one launch (start us, length us, event | category | flops | bytes accessed | tf_op | source)
XLA Modules:
  0.0 164.1 jit_solution(6266151872323987902)
XLA Ops:
  0.6 160.3 %shard_map.140 = (bf16[8,4096]{1,0:T(8,128)(2,1)}, bf16[64,2048]{1,0:T(8,128)(2,1)}) custom-call(s32[8]{0:T(128)} %lengths_ref.1, bf16[8,4096]{1,0:T(8,128)(2,1)} %queries_ref.1, bf16[8,64,512]{2,1,0:T(8,128)(2,1)} %keys_ref.1, bf16[8,64,512]{2,1,0:T(8,128)(2,1)} %values_ref.1, bf16[8,512]{1,0:T(8,128)(2,1)} %new_key_ref.1, bf16[8,512]{1,0:T(8,128)(2,1)} %new_value_ref.1, ...), custom_call_target="tpu_custom_call" | custom-call | tf_op jit(solution)/shard_map/pallas_call | solution.py:988
  161.0 1.5 copy.17
  162.5 1.7 %copy.18 = bf16[64,2048]{1,0:T(8,128)(2,1)} copy(bf16[64,2048]{1,0:T(8,128)(2,1)} %get-tuple-element.5) | data formatting | bytes 524288

commit v3 on v2

--- a/solution.py
+++ b/solution.py
@@ -71,6 +71,8 @@
 AHEAD = 4
 NEAR = 4
 LAG = 2
+FUSED_AHEAD = 2
+ROW_SPACING = 2
 
 
 def greet(targets):
@@ -572,6 +574,13 @@
     )
     rows[me, :, width:] = shares.astype(jnp.bfloat16)
 
+    @pl.loop(0, count)
+    def _(e):
+        for m in range(2):
+            loading(m, e).wait()
+            turned = load[m, e].T.reshape(count, share, depth)
+            stage[m, :, pl.ds(pl.multiple_of(e * share, share), share), :] = turned
+
     pl.semaphore_wait(barrier, len(peers))
 
     def remote(src, dst, send, recv, target):
@@ -663,13 +672,6 @@
         if r >= NEAR:
             onward(r).start()
 
-    @pl.loop(0, count)
-    def _(e):
-        for m in range(2):
-            loading(m, e).wait()
-            turned = load[m, e].T.reshape(count, share, depth)
-            stage[m, :, pl.ds(pl.multiple_of(e * share, share), share), :] = turned
-
     for m in range(2):
         wt[m, :, lanes_of(me)] = stage[m, me]
 
@@ -680,27 +682,25 @@
     blocks = chunk // row_count
 
     def accumulate(r, first):
+        base = pl.multiple_of(((me ^ r) // 2) * (2 * depth), 2 * depth)
+
+        def add_product(m):
+            @pl.loop(0, chunks)
+            def _(c):
+                x = rows[pl.ds(c * blocks, blocks), :, pl.ds(base, 2 * depth)].reshape(chunk, 2 * depth)
+                weight = wt[m, :, pl.ds(base, 2 * depth)]
+                product = lax.dot_general(x, weight, by_last, preferred_element_type=jnp.float32)
+                at = pl.ds(pl.multiple_of(c * chunk, chunk), chunk)
+                if first:
+                    acc[m, at, :] = product
+                else:
+                    acc[m, at, :] = acc[m, at, :] + product
+
+        add_product(group)
         for q in (r, r ^ 1):
             if q >= NEAR:
                 onward(q).wait_recv()
-        base = pl.multiple_of(((me ^ r) // 2) * (2 * depth), 2 * depth)
-
-        @pl.loop(0, 2 * tiles)
-        def _(step):
-            m, n = step // tiles, step % tiles
-            weight = wt[m, pl.ds(pl.multiple_of(n * tile, tile), tile), pl.ds(base, 2 * depth)]
-
-            @pl.loop(0, chunks)
-            def _(c):
-                x = rows[pl.ds(c * blocks, blocks), :, pl.ds(base, 2 * depth)].reshape(chunk, 2 * depth)
-                product = lax.dot_general(
-                    x, weight, by_last, preferred_element_type=jnp.float32
-                )
-                at = pl.ds(pl.multiple_of(c * chunk, chunk), chunk)
-                if first:
-                    acc[step, at, :] = product
-                else:
-                    acc[step, at, :] = acc[step, at, :] + product
+        add_product(other_group)
 
     def attend_here():
         for copy in small[4:9]:
@@ -744,47 +744,59 @@
                     h * seq_count : (h + 1) * seq_count, :
                 ].astype(attended_ref.dtype)
 
-    half = count // 2
-    order = [r for i in range(half) for r in ((half + i, i) if i else (half,))]
-    passed, pending, done = {0}, [], 0
-    side_at = 2 * line
-
-    def after(i):
-        nonlocal done
-        r = order[i]
+    by_distance = [[NEAR * d + i for i in range(NEAR)] for d in range(1, line)]
+    by_distance = by_distance[1:] + by_distance[:1]
+    far = []
+    for i in range(0, NEAR, 2):
+        pairs = [group_of[i : i + 2] for group_of in by_distance]
+        far += [pair[0] for pair in pairs[:-1]] + [pairs[0][1], pairs[-1][0]]
+        far += [pair[1] for pair in pairs[1:]]
+    order = list(range(1, NEAR)) + far
+    row_at = [1 + ROW_SPACING * step for step in range(line - 1)]
+    side_at = row_at[-1] + 1
+    compute_from = side_at + 1
+
+    for r in range(1, NEAR):
+        start_weight(r)
+
+    complete = []
+
+    def advance(i):
+        r = far[i]
         pass_on(r)
-        passed.add(r)
-        if r ^ 1 in passed:
-            pending.append((i, r))
-
-    started_rows = False
+        if r ^ 1 in far[:i]:
+            complete.append((i, r))
+
+    def rows_and_near():
+        rows_ready()
+        for r in range(1, NEAR):
+            pass_on(r)
+        accumulate(0, True)
+        for r in range(2, NEAR, 2):
+            accumulate(r, False)
 
     def compute(i):
-        nonlocal done, started_rows
-        while pending and (pending[0][0] + LAG <= i):
-            _, r = pending.pop(0)
-            if not started_rows:
-                rows_ready()
-                started_rows = True
-            accumulate(r, done == 0)
-            done += 1
-
-    for i, r in enumerate(order):
-        start_weight(r)
-        if i % 2 == 1 and i // 2 < line - 1:
-            line_step(i // 2)
+        while complete and complete[0][0] + LAG <= i:
+            accumulate(complete.pop(0)[1], False)
+
+    for i, r in enumerate(far):
+        if i in row_at:
+            line_step(row_at.index(i))
         if i == side_at:
             side_step()
-        if i == AHEAD - 1:
+        start_weight(r)
+        if i == 0:
             attend_here()
-        if i >= AHEAD:
-            after(i - AHEAD)
-            if i > side_at:
-                compute(i - AHEAD)
-    for i in range(len(order) - AHEAD, len(order)):
-        after(i)
+        if i == compute_from:
+            rows_and_near()
+        if i >= FUSED_AHEAD:
+            advance(i - FUSED_AHEAD)
+        if i > compute_from:
+            compute(i - FUSED_AHEAD)
+    for i in range(len(far) - FUSED_AHEAD, len(far)):
+        advance(i)
         compute(i)
-    compute(len(order) + LAG)
+    compute(len(far) + LAG)
 
     spread_at = lax.broadcasted_iota(jnp.int32, (128, total_f), 0)
     column = lax.broadcasted_iota(jnp.int32, (128, total_f), 1)
@@ -817,17 +829,19 @@
             here = pl.ds(pl.multiple_of(block * row_count, row_count), row_count)
             there = pl.ds(pl.multiple_of(b * row_count, row_count), row_count)
             for n in range(tiles):
-                gate_proj = acc[n, here, :]
-                up_proj = acc[tiles + n, here, :]
                 columns = slice(n * tile, (n + 1) * tile)
+                gate_proj = acc[0, here, columns]
+                up_proj = acc[1, here, columns]
                 hidden = gate_proj / (1.0 + jnp.exp(-gate_proj)) * up_proj * mix[:, columns]
                 units[there, columns] = hidden.astype(units.dtype)
 
-        @pl.loop(0, width // tile)
+        wide = 2 * tile
+
+        @pl.loop(0, width // wide)
         def _(n):
-            columns = pl.ds(pl.multiple_of(n * tile, tile), tile)
+            columns = pl.ds(pl.multiple_of(n * wide, wide), wide)
             product = jnp.dot(units[...], down[:, columns], preferred_element_type=jnp.float32)
-            part[pl.ds(at * 4, 4), :, columns] = product.astype(part.dtype).reshape(4, row_count, tile)
+            part[pl.ds(at * 4, 4), :, columns] = product.astype(part.dtype).reshape(4, row_count, wide)
 
     def add(target, *sources):
         @pl.loop(0, row_count // 16)
@@ -866,27 +880,30 @@
         add(side_out.at[at], *held(at, side ^ 1, first))
         line_copy(0, at).start()
 
-    def step_along(at, kinds, sources):
+    def step_along(at, kinds, sources, starting, passing):
         for kind, has_source, moving in ((kinds[0], has_down, at > layer), (kinds[1], has_up, at < layer)):
-            @pl.when(jnp.logical_and(moving, has_source))
-            def _():
+            def pass_sum():
                 line_copy(kind, at).wait_recv()
                 sources(kind, True)
                 line_copy(kind, at).start()
 
-            @pl.when(jnp.logical_and(moving, jnp.logical_not(has_source)))
-            def _():
+            def start_sum():
                 sources(kind, False)
                 line_copy(kind, at).start()
 
-    def early(at):
+            if passing:
+                pl.when(jnp.logical_and(moving, has_source))(pass_sum)
+            if starting:
+                pl.when(jnp.logical_and(moving, jnp.logical_not(has_source)))(start_sum)
+
+    def early(at, starting):
         def sources(kind, arriving):
             out, arrived = ((early_up_out, early_up_in), (early_down_out, early_down_in))[kind - 1]
             for y in range(2):
                 more = (arrived.at[at, y],) if arriving else ()
                 add(out.at[at, y], *held(at, y, second), *more)
 
-        step_along(at, (1, 2), sources)
+        step_along(at, (1, 2), sources, starting, not starting)
 
     def late(at):
         line_copy(0, at).wait_recv()
@@ -896,7 +913,7 @@
             more = (arrived.at[at],) if arriving else ()
             add(out.at[at], *held(at, side, first), side_in.at[at], *more)
 
-        step_along(at, (3, 4), sources)
+        step_along(at, (3, 4), sources, True, True)
 
     def arrived_from(kinds, act):
         @pl.when(has_down)
@@ -918,9 +935,10 @@
         core_copy(at, side).start()
         if j:
             to_side(turn(j - 1))
+            early(turn(j - 1), True)
     to_side(turn(line - 1))
     for j in range(line - 1):
-        early(turn(j))
+        early(turn(j), False)
     for j in range(line - 1):
         late(turn(j))
     line_copy(0, layer).wait_recv()
@@ -976,7 +994,7 @@
     count, depth, total_f = gate_train.shape
     row_count, width = hidden_in.shape
     line = count // 4
-    first_columns = pl.cdiv(width * 6, 10 * 128) * 128
+    first_columns = width * 13 // (16 * 128) * 128
     second_columns = width - first_columns
     anywhere = pl.BlockSpec(memory_space=pl.ANY)
     near = pl.BlockSpec(memory_space=pltpu.VMEM)
@@ -1000,7 +1018,7 @@
             held(2, count, total_f, depth),
             held(2, total_f, count * depth),
             held(count, row_count, width + 128),
-            pltpu.VMEM((2 * total_f // 256, count * row_count, 256), jnp.float32),
+            pltpu.VMEM((2, count * row_count, total_f), jnp.float32),
             held(4 * row_count, total_f),
             held(count, row_count, width),
             held(2 * line, row_count, width),

time: 164 us -> 141 us (0.86)
  Pallas kernels: 160 us -> 137 us
    pallas_call x1, Pallas kernels: 160 us -> 137 us  [fused(): pl.pallas_call(functools.partial(fused_kernel, count, first_columns), out...]
where the time goes in v3:
time: 141 us
  Pallas kernels  137 us (97%)
  local copies, waits for them, and re-layouts  3.14 us (2%)
    pallas_call x1, Pallas kernels, fused(): pl.pallas_call(functools.partial(fused_kernel, count, first_columns), out...  137 us
    unnamed x2, local copies, waits for them, and re-layouts  3.14 us

profile of v3, /device:TPU:0, one launch (start us, length us, event | category | flops | bytes accessed | tf_op | source)
XLA Modules:
  0.0 140.5 jit_solution(15927552085191781293)
XLA Ops:
  0.6 136.7 %shard_map.140 = (bf16[8,4096]{1,0:T(8,128)(2,1)}, bf16[64,2048]{1,0:T(8,128)(2,1)}) custom-call(s32[8]{0:T(128)} %lengths_ref.1, bf16[8,4096]{1,0:T(8,128)(2,1)} %queries_ref.1, bf16[8,64,512]{2,1,0:T(8,128)(2,1)} %keys_ref.1, bf16[8,64,512]{2,1,0:T(8,128)(2,1)} %values_ref.1, bf16[8,512]{1,0:T(8,128)(2,1)} %new_key_ref.1, bf16[8,512]{1,0:T(8,128)(2,1)} %new_value_ref.1, ...), custom_call_target="tpu_custom_call" | custom-call | tf_op jit(solution)/shard_map/pallas_call | solution.py:1006
  137.4 1.5 %copy.17 = bf16[8,4096]{1,0:T(8,128)(2,1)} copy(bf16[8,4096]{1,0:T(8,128)(2,1)} %get-tuple-element.4) | data formatting | bytes 131072
  138.8 1.7 %copy.18 = bf16[64,2048]{1,0:T(8,128)(2,1)} copy(bf16[64,2048]{1,0:T(8,128)(2,1)} %get-tuple-element.5) | data formatting | bytes 524288

commit v4 on v3

--- a/solution.py
+++ b/solution.py
@@ -71,8 +71,12 @@
 AHEAD = 4
 NEAR = 4
 LAG = 2
-FUSED_AHEAD = 2
-ROW_SPACING = 2
+FUSED_AHEAD = 4
+ROW_FIRST = 2
+ROW_SPACING = 4
+SIDE_AFTER = 2
+PIECES = 2
+FIRST = 2
 
 
 def greet(targets):
@@ -540,6 +544,54 @@
     for peer in peers:
         pl.semaphore_signal(barrier, inc=1, device_id=peer, device_id_type=MESH)
 
+    @pl.loop(0, count)
+    def _(e):
+        for m in range(2):
+            loading(m, e).wait()
+            turned = load[m, e].T.reshape(count, share, depth)
+            stage[m, :, pl.ds(pl.multiple_of(e * share, share), share), :] = turned
+
+    pl.semaphore_wait(barrier, len(peers))
+
+    def remote(src, dst, send, recv, target):
+        return pltpu.make_async_remote_copy(
+            src_ref=src, dst_ref=dst, send_sem=send, recv_sem=recv, device_id=target, device_id_type=MESH
+        )
+
+    pieces = PIECES
+    piece_rows = total_f // pieces
+
+    def lanes_of(owner):
+        return pl.ds(pl.multiple_of(owner * depth, depth), depth)
+
+    def rows_of(piece):
+        return pl.ds(piece * piece_rows, piece_rows)
+
+    def near_copy(m, r):
+        return remote(
+            stage.at[m, me ^ r], wt.at[m, :, lanes_of(me)], send_w.at[m, r], recv_w.at[m, r], (group, me ^ r)
+        )
+
+    def far_copy(r, piece):
+        return remote(
+            stage.at[group, me ^ r, rows_of(piece)], wt.at[group, rows_of(piece), lanes_of(me)],
+            send_w.at[piece, r], recv_w.at[piece, r], (group, me ^ r),
+        )
+
+    def onward(r, piece):
+        ref = wt.at[group, rows_of(piece), lanes_of(me ^ r)]
+        return remote(ref, ref, send_x.at[piece, r], recv_x.at[piece, r], (other_group, me))
+
+    by_distance = [[NEAR * d + i for i in range(NEAR)] for d in range(1, line)]
+    by_distance = by_distance[1:] + by_distance[:1]
+    far = []
+    for i in range(0, NEAR, 2):
+        pairs = [group_of[i : i + 2] for group_of in by_distance]
+        far += [pair[0] for pair in pairs[:-1]] + [pairs[0][1], pairs[-1][0]]
+        far += [pair[1] for pair in pairs[1:]]
+    items = [(r, piece) for r in far for piece in range(pieces)]
+    for item in items[:FIRST]:
+        far_copy(*item).start()
     for copy in small[:4]:
         copy.wait()
     values = hid_ref[...].astype(jnp.float32)
@@ -574,20 +626,6 @@
     )
     rows[me, :, width:] = shares.astype(jnp.bfloat16)
 
-    @pl.loop(0, count)
-    def _(e):
-        for m in range(2):
-            loading(m, e).wait()
-            turned = load[m, e].T.reshape(count, share, depth)
-            stage[m, :, pl.ds(pl.multiple_of(e * share, share), share), :] = turned
-
-    pl.semaphore_wait(barrier, len(peers))
-
-    def remote(src, dst, send, recv, target):
-        return pltpu.make_async_remote_copy(
-            src_ref=src, dst_ref=dst, send_sem=send, recv_sem=recv, device_id=target, device_id_type=MESH
-        )
-
     def row_copy(kind, block, target):
         return remote(
             rows.at[block], rows.at[block], send_rows.at[kind, block], recv_rows.at[block], (group, target)
@@ -644,33 +682,6 @@
         for index in range(line):
             for y in range(2):
                 row_wait(4 * index + 2 * y + (lax.rem(me, 2) ^ 1))
-
-    def lanes_of(owner):
-        return pl.ds(pl.multiple_of(owner * depth, depth), depth)
-
-    def across(m, r):
-        target = me ^ r
-        index = m if r < NEAR else group
-        slot = m if r < NEAR else 0
-        return remote(
-            stage.at[index, target], wt.at[index, :, lanes_of(me)],
-            send_w.at[slot, r], recv_w.at[slot, r], (group, target),
-        )
-
-    def onward(r):
-        held = me ^ r
-        ref = wt.at[group, :, lanes_of(held)]
-        return remote(ref, ref, send_x.at[r], recv_x.at[r], (other_group, me))
-
-    def start_weight(r):
-        for m in range(2 if r < NEAR else 1):
-            across(m, r).start()
-
-    def pass_on(r):
-        for m in range(2 if r < NEAR else 1):
-            across(m, r).wait_recv()
-        if r >= NEAR:
-            onward(r).start()
 
     for m in range(2):
         wt[m, :, lanes_of(me)] = stage[m, me]
@@ -698,8 +709,8 @@
 
         add_product(group)
         for q in (r, r ^ 1):
-            if q >= NEAR:
-                onward(q).wait_recv()
+            for piece in range(pieces if q >= NEAR else 0):
+                onward(q, piece).wait_recv()
         add_product(other_group)
 
     def attend_here():
@@ -744,33 +755,28 @@
                     h * seq_count : (h + 1) * seq_count, :
                 ].astype(attended_ref.dtype)
 
-    by_distance = [[NEAR * d + i for i in range(NEAR)] for d in range(1, line)]
-    by_distance = by_distance[1:] + by_distance[:1]
-    far = []
-    for i in range(0, NEAR, 2):
-        pairs = [group_of[i : i + 2] for group_of in by_distance]
-        far += [pair[0] for pair in pairs[:-1]] + [pairs[0][1], pairs[-1][0]]
-        far += [pair[1] for pair in pairs[1:]]
-    order = list(range(1, NEAR)) + far
-    row_at = [1 + ROW_SPACING * step for step in range(line - 1)]
-    side_at = row_at[-1] + 1
-    compute_from = side_at + 1
+    row_at = [ROW_FIRST + ROW_SPACING * step for step in range(line - 1)]
+    side_at = row_at[-1] + SIDE_AFTER
+    compute_from = side_at + SIDE_AFTER
 
     for r in range(1, NEAR):
-        start_weight(r)
+        for m in range(2):
+            near_copy(m, r).start()
 
     complete = []
 
     def advance(i):
-        r = far[i]
-        pass_on(r)
-        if r ^ 1 in far[:i]:
+        r, piece = items[i]
+        far_copy(r, piece).wait_recv()
+        onward(r, piece).start()
+        if all((r ^ 1, q) in items[:i] for q in range(pieces)) and piece == pieces - 1:
             complete.append((i, r))
 
     def rows_and_near():
         rows_ready()
         for r in range(1, NEAR):
-            pass_on(r)
+            for m in range(2):
+                near_copy(m, r).wait_recv()
         accumulate(0, True)
         for r in range(2, NEAR, 2):
             accumulate(r, False)
@@ -779,12 +785,13 @@
         while complete and complete[0][0] + LAG <= i:
             accumulate(complete.pop(0)[1], False)
 
-    for i, r in enumerate(far):
+    for i, item in enumerate(items):
         if i in row_at:
             line_step(row_at.index(i))
         if i == side_at:
             side_step()
-        start_weight(r)
+        if i >= FIRST:
+            far_copy(*item).start()
         if i == 0:
             attend_here()
         if i == compute_from:
@@ -793,10 +800,10 @@
             advance(i - FUSED_AHEAD)
         if i > compute_from:
             compute(i - FUSED_AHEAD)
-    for i in range(len(far) - FUSED_AHEAD, len(far)):
+    for i in range(len(items) - FUSED_AHEAD, len(items)):
         advance(i)
         compute(i)
-    compute(len(far) + LAG)
+    compute(len(items) + LAG)
 
     spread_at = lax.broadcasted_iota(jnp.int32, (128, total_f), 0)
     column = lax.broadcasted_iota(jnp.int32, (128, total_f), 1)
@@ -966,11 +973,12 @@
         for up_kind in (1, 3):
             pl.when(at > layer)(line_copy(up_kind, at).wait_send)
             pl.when(at < layer)(line_copy(up_kind + 1, at).wait_send)
-    for r in order:
-        for m in range(2 if r < NEAR else 1):
-            across(m, r).wait_send()
-        if r >= NEAR:
-            onward(r).wait_send()
+    for r in range(1, NEAR):
+        for m in range(2):
+            near_copy(m, r).wait_send()
+    for item in items:
+        far_copy(*item).wait_send()
+        onward(*item).wait_send()
     for index in range(line):
         block = lax.rem(me, 4) + 4 * index
 
@@ -1006,8 +1014,8 @@
     return pl.pallas_call(
         functools.partial(fused_kernel, count, first_columns),
         out_shape=[
-            jax.ShapeDtypeStruct(queries.shape, jnp.bfloat16),
-            jax.ShapeDtypeStruct((row_count, width), jnp.bfloat16),
+            pltpu.VMEM(queries.shape, jnp.bfloat16),
+            pltpu.VMEM((row_count, width), jnp.bfloat16),
         ],
         in_specs=[pl.BlockSpec(memory_space=pltpu.SMEM)] + [anywhere] * 12,
         out_specs=[near, near],
@@ -1026,7 +1034,7 @@
             *[held(line, 2, row_count, second_columns)] * 4,
             *[held(line, row_count, first_columns)] * 4,
             held(row_count, second_columns), held(row_count, second_columns),
-            DMA((10,)), DMA((2, count)), DMA((2, count)), DMA((2, count)), DMA((count,)), DMA((count,)),
+            DMA((10,)), DMA((2, count)), *[DMA((max(2, PIECES), count))] * 2, *[DMA((PIECES, count))] * 2,
             DMA((4, count)), DMA((count,)),
             DMA((2 * line,)), DMA((2 * line,)), DMA((5, line)), DMA((5, line)), DMA((1,)), DMA((1,)),
         ],

time: 141 us -> 137 us (0.972)
  Pallas kernels: 137 us -> 135 us
  local copies, waits for them, and re-layouts: 3.14 us -> 1.33 us
    unnamed x2, local copies, waits for them, and re-layouts: 3.14 us -> 1.33 us
where the time goes in v4:
time: 137 us
  Pallas kernels  135 us (99%)
    pallas_call x1, Pallas kernels, fused(): pl.pallas_call(functools.partial(fused_kernel, count, first_columns), out...  135 us

profile of v4, /device:TPU:0, one launch (start us, length us, event | category | flops | bytes accessed | tf_op | source)
XLA Modules:
  0.0 137.3 jit_solution(11065234879938085805)
XLA Ops:
  0.6 135.4 %shard_map.140 = (bf16[8,4096]{1,0:T(8,128)(2,1)S(1)}, bf16[64,2048]{1,0:T(8,128)(2,1)S(1)}) custom-call(s32[8]{0:T(128)} %lengths_ref.1, bf16[8,4096]{1,0:T(8,128)(2,1)} %queries_ref.1, bf16[8,64,512]{2,1,0:T(8,128)(2,1)} %keys_ref.1, bf16[8,64,512]{2,1,0:T(8,128)(2,1)} %values_ref.1, bf16[8,512]{1,0:T(8,128)(2,1)} %new_key_ref.1, ...), custom_call_target="tpu_custom_call" | custom-call | tf_op jit(solution)/shard_map/pallas_call | solution.py:1014
  136.0 0.6 copy.17
  136.6 0.7 copy.18

commit v5 on v4

--- a/solution.py
+++ b/solution.py
@@ -755,7 +755,7 @@
                     h * seq_count : (h + 1) * seq_count, :
                 ].astype(attended_ref.dtype)
 
-    row_at = [ROW_FIRST + ROW_SPACING * step for step in range(line - 1)]
+    row_at = [ROW_FIRST + ROW_SPACING * step - step // 2 for step in range(line - 1)]
     side_at = row_at[-1] + SIDE_AFTER
     compute_from = side_at + SIDE_AFTER
 

time: 137 us -> 142 us (1.036)
  Pallas kernels: 135 us -> 140 us
    pallas_call x1, Pallas kernels: 135 us -> 140 us  [fused(): pl.pallas_call(functools.partial(fused_kernel, count, first_columns), out...]
where the time goes in v5:
time: 142 us
  Pallas kernels  140 us (99%)
    pallas_call x1, Pallas kernels, fused(): pl.pallas_call(functools.partial(fused_kernel, count, first_columns), out...  140 us

profile of v5, /device:TPU:0, one launch (start us, length us, event | category | flops | bytes accessed | tf_op | source)
XLA Modules:
  0.0 141.6 jit_solution(18007637773830871508)
XLA Ops:
  0.6 139.7 %shard_map.140 = (bf16[8,4096]{1,0:T(8,128)(2,1)S(1)}, bf16[64,2048]{1,0:T(8,128)(2,1)S(1)}) custom-call(s32[8]{0:T(128)} %lengths_ref.1, bf16[8,4096]{1,0:T(8,128)(2,1)} %queries_ref.1, bf16[8,64,512]{2,1,0:T(8,128)(2,1)} %keys_ref.1, bf16[8,64,512]{2,1,0:T(8,128)(2,1)} %values_ref.1, bf16[8,512]{1,0:T(8,128)(2,1)} %new_key_ref.1, ...), custom_call_target="tpu_custom_call" | custom-call | tf_op jit(solution)/shard_map/pallas_call | solution.py:1014
  140.3 0.6 copy.17
  140.9 0.7 copy.18
